TPU v7x, 32 devices: a whole 2x2x4 slice. The times are simulated.
32 devices in a mesh: gx: 2 (over y), gy: 4 (over z), gz: 4 (over x, core).
Axes of the slice: x: 2, y: 2, z: 4, core: 2. Of those that a mesh axis runs over, the one named last changes fastest.
Arguments:
- concentration: float32 [32, 256, 512], P('gx', 'gy', 'gz'), may hold values from -6 to 6
- speed: float32 [3, 32, 256, 512], P(None, 'gx', 'gy', 'gz'), may hold values from 0.1 to 1
- signs: int32 [3, 32, 256, 512], P(None, 'gx', 'gy', 'gz'), may hold values from 0 to 1
- diffusivity: float32 [32, 256, 512], P('gx', 'gy', 'gz'), may hold values from 0.02 to 0.12
- shear: int32 [1], replicated, may hold values from 0 to 255
Outputs:
- final_field: float32 [32, 256, 512], P('gx', 'gy', 'gz')
All inputs are finite; a program needn't handle non-finite values.
Results may differ from a plain program's by a relative error of at most 0.00002.
Values sent between devices are 32-bit elements; how exact they have to be, the bound alone decides.
A program may use at most 64 MiB of HBM per device.

v0:
```python
import functools

import jax
import jax.numpy as jnp
from jax import lax
from jax.experimental import pallas as pl
from jax.experimental.pallas import tpu as pltpu
from jax.sharding import PartitionSpec as P

STEPS = 8
time_step = 0.25
PAD = 8
MESH = pl.DeviceIdType.MESH


def kernel(
    hops, count_x, count_y, count_z,
    shear, conc, speed, signs, diff, out,
    field, coef, v_buf, s_buf, d_buf, low0, low1, high0, high1, y_out, y_in, z_out, z_in,
    load_sem, send_sem, recv_sem,
):
    nx, rows, lanes = conc.shape
    blocks = rows // 8
    span = 2 * nx
    per = lanes // span
    gx, gy, gz = (lax.axis_index(name) for name in ("gx", "gy", "gz"))
    low, high = (low0, low1), (high0, high1)
    first, last = gx == 0, gx == count_x - 1
    body_rows = pl.ds(PAD, rows)

    def at(x, y):
        return {"gx": x, "gy": lax.rem(y + 2 * count_y, count_y)}

    up = (
        at(jnp.where(last, 0, gx + 1), gy - jnp.where(last, hops, 0)),
        at(0, gy - hops - 1),
    )
    down = (
        at(jnp.where(first, count_x - 1, gx - 1), gy + jnp.where(first, hops + 1, 0)),
        at(count_x - 1, gy + hops),
    )
    before_y, after_y = at(gx, gy - 1), at(gx, gy + 1)
    before_z = {"gz": lax.rem(gz + count_z - 1, count_z)}
    after_z = {"gz": lax.rem(gz + 1, count_z)}

    def remote(p, role, source, target, device):
        return pltpu.make_async_remote_copy(
            src_ref=source, dst_ref=target,
            send_sem=send_sem.at[p, role], recv_sem=recv_sem.at[p, role],
            device_id=device, device_id_type=MESH,
        )

    def copies(p):
        top = field.at[p, nx - 1, body_rows]
        bottom = field.at[p, 0, body_rows]
        halves = (pl.ds(0, rows), pl.ds(rows, rows))
        return (
            remote(p, 0, top, low[p].at[halves[0]], up[0]),
            remote(p, 1, top, low[p].at[halves[1]], up[1]),
            remote(p, 2, bottom, high[p].at[halves[0]], down[0]),
            remote(p, 3, bottom, high[p].at[halves[1]], down[1]),
            remote(p, 4, y_out.at[p, 0], y_in.at[p, 1], before_y),
            remote(p, 5, y_out.at[p, 1], y_in.at[p, 0], after_y),
            remote(p, 6, z_out.at[p], z_in.at[p, 1], before_z),
            remote(p, 7, z_out.at[p], z_in.at[p, 0], after_z),
        )

    def send(p):
        c = copies(p)
        pl.when(last)(c[1].start)
        pl.when(first)(c[3].start)
        for role in (0, 2, 4, 5, 6, 7):
            c[role].start()

    lane = lax.broadcasted_iota(jnp.int32, (8, lanes), 1)
    even = lane % 2 == 0

    def turn(value, amount):
        return pltpu.roll(value, lax.rem(amount + 2 * lanes, lanes), 1)

    def pack(packed, block, x, value):
        spot = span * (block % per) + 2 * x
        moved = turn(value, spot + 1)
        group = block // per
        old = packed[group]
        new = jnp.where((lane == spot) | (lane == spot + 1), moved, old)
        return packed[:group] + (new,) + packed[group + 1 :]

    def put_edges(q, x, packed):
        y_out[q, 0, pl.ds(x, 1)] = field[q, x, pl.ds(PAD, 1)]
        y_out[q, 1, pl.ds(x, 1)] = field[q, x, pl.ds(PAD + rows - 1, 1)]

    def store_packed(q, packed):
        for group, value in enumerate(packed):
            z_out[q, group] = value

    groups = blocks // per
    nothing = tuple(jnp.zeros((8, lanes), jnp.float32) for _ in range(groups))

    loads = (
        pltpu.make_async_copy(conc, field.at[0, :, body_rows], load_sem.at[0]),
        pltpu.make_async_copy(diff, d_buf, load_sem.at[1]),
        pltpu.make_async_copy(speed, v_buf, load_sem.at[2]),
        pltpu.make_async_copy(signs, s_buf, load_sem.at[3]),
    )
    for load in loads:
        load.start()

    barrier = pltpu.get_barrier_semaphore()

    def greet(device):
        pl.semaphore_signal(barrier, inc=1, device_id=device, device_id_type=MESH)

    for device in (up[0], down[0], before_y, after_y, before_z, after_z):
        greet(device)
    pl.when(last)(lambda: greet(up[1]))
    pl.when(first)(lambda: greet(down[1]))
    pl.semaphore_wait(barrier, 6 + jnp.where(first | last, 1, 0))

    loads[0].wait()

    def first_pack(x, packed):
        for block in range(blocks):
            packed = pack(packed, block, x, field[0, x, pl.ds(PAD + 8 * block, 8)])
        put_edges(0, x, packed)
        return packed

    store_packed(0, lax.fori_loop(0, nx, first_pack, nothing))
    send(0)
    for load in loads[1:]:
        load.wait()

    def weigh(x, carry):
        d = time_step * d_buf[x]
        centre = 1.0 - 6.0 * d
        for axis in range(3):
            v = time_step * v_buf[axis, x]
            forward = s_buf[axis, x] > 0
            below = jnp.where(forward, v, 0.0)
            above = v - below
            coef[1 + 2 * axis, x] = d + below
            coef[2 + 2 * axis, x] = d - above
            centre = centre - below + above
        coef[0, x] = centre
        return carry

    lax.fori_loop(0, nx, weigh, 0)

    residue = lax.rem(shear[0], rows)
    low_start = jnp.where(first, residue, 0)
    high_start = jnp.where(last, rows - residue, 0)

    def step(p, more):
        q = 1 - p
        c = copies(p)
        for role in (4, 5, 6, 7):
            c[role].wait_recv()
        for x in range(nx):
            field[p, x, pl.ds(PAD - 1, 1)] = y_in[p, 0, pl.ds(x, 1)]
            field[p, x, pl.ds(PAD + rows, 1)] = y_in[p, 1, pl.ds(x, 1)]
        sides = tuple(
            jnp.where(even, z_in[p, 0, group], turn(z_in[p, 1, group], -2))
            for group in range(groups)
        )

        def plane(x, packed, lower, upper):
            for block in range(blocks):
                start = PAD + 8 * block
                part = pl.ds(8 * block, 8)
                here = field[p, x, pl.ds(start, 8)]
                side = turn(sides[block // per], -(span * (block % per) + 2 * x))
                z_minus = jnp.where(lane == 0, side, turn(here, 1))
                z_plus = jnp.where(lane == lanes - 1, side, turn(here, -1))
                total = (
                    (coef[0, x, part] * here + coef[1, x, part] * lower(block))
                    + (coef[2, x, part] * upper(block)
                       + coef[3, x, part] * field[p, x, pl.ds(start - 1, 8)])
                ) + (
                    (coef[4, x, part] * field[p, x, pl.ds(start + 1, 8)]
                     + coef[5, x, part] * z_minus)
                    + coef[6, x, part] * z_plus
                )
                field[q, x, pl.ds(start, 8)] = total
                packed = pack(packed, block, x, total)
            put_edges(q, x, packed)
            return packed

        def from_field(x):
            return lambda block: field[p, x, pl.ds(PAD + 8 * block, 8)]

        packed = lax.fori_loop(
            1, nx - 1,
            lambda x, packed: plane(x, packed, from_field(x - 1), from_field(x + 1)),
            nothing,
        )
        c[0].wait_recv()
        c[2].wait_recv()
        pl.when(first)(c[1].wait_recv)
        pl.when(last)(c[3].wait_recv)
        packed = plane(
            0, packed, lambda block: low[p][pl.ds(low_start + 8 * block, 8)], from_field(1)
        )
        packed = plane(
            nx - 1, packed, from_field(nx - 2),
            lambda block: high[p][pl.ds(high_start + 8 * block, 8)],
        )
        store_packed(q, packed)
        for role in (0, 2, 4, 5, 6, 7):
            c[role].wait_send()
        pl.when(last)(c[1].wait_send)
        pl.when(first)(c[3].wait_send)
        if more is None:
            send(q)
        else:
            pl.when(more)(lambda: send(q))

    def pair(t, carry):
        step(0, None)
        step(1, t < STEPS // 2 - 1)
        return carry

    lax.fori_loop(0, STEPS // 2, pair, 0)
    store = pltpu.make_async_copy(field.at[STEPS % 2, :, body_rows], out, load_sem.at[0])
    store.start()
    store.wait()


def run(hops, counts, shear, conc, speed, signs, diff):
    nx, rows, lanes = conc.shape
    f32 = jnp.float32
    groups = (rows // 8) // (lanes // (2 * nx))
    anywhere = pl.BlockSpec(memory_space=pl.ANY)
    return pl.pallas_call(
        functools.partial(kernel, hops, *counts),
        name=f"slide{hops}",
        out_shape=jax.ShapeDtypeStruct(conc.shape, f32),
        in_specs=[pl.BlockSpec(memory_space=pltpu.SMEM)] + [anywhere] * 4,
        out_specs=anywhere,
        scratch_shapes=[
            pltpu.VMEM((2, nx, rows + 2 * PAD, lanes), f32),
            pltpu.VMEM((7, nx, rows, lanes), f32),
            pltpu.VMEM((3, nx, rows, lanes), f32),
            pltpu.VMEM((3, nx, rows, lanes), jnp.int32),
            pltpu.VMEM((nx, rows, lanes), f32),
            pltpu.VMEM((2 * rows, lanes), f32),
            pltpu.VMEM((2 * rows, lanes), f32),
            pltpu.VMEM((2 * rows, lanes), f32),
            pltpu.VMEM((2 * rows, lanes), f32),
            pltpu.VMEM((2, 2, nx, lanes), f32),
            pltpu.VMEM((2, 2, nx, lanes), f32),
            pltpu.VMEM((2, groups, 8, lanes), f32),
            pltpu.VMEM((2, 2, groups, 8, lanes), f32),
            pltpu.SemaphoreType.DMA((4,)),
            pltpu.SemaphoreType.DMA((2, 8)),
            pltpu.SemaphoreType.DMA((2, 8)),
        ],
        compiler_params=pltpu.CompilerParams(collective_id=hops, has_side_effects=True),
    )(shear, conc, speed, signs, diff)


def body(concentration, speed, signs, diffusivity, shear):
    counts = tuple(lax.axis_size(name) for name in ("gx", "gy", "gz"))
    rows = concentration.shape[1]
    branches = [functools.partial(run, hops, counts) for hops in range(counts[1])]
    return lax.switch(
        lax.div(shear[0], rows), branches, shear, concentration, speed, signs, diffusivity
    )


def solution(mesh):
    placed = (
        P("gx", "gy", "gz"),
        P(None, "gx", "gy", "gz"),
        P(None, "gx", "gy", "gz"),
        P("gx", "gy", "gz"),
        P(),
    )
    return jax.shard_map(
        body, mesh=mesh, in_specs=placed, out_specs=P("gx", "gy", "gz"), check_vma=False
    )
```

profile of v0, /device:TPU:0, one launch (start us, length us, event | category | flops | bytes accessed | tf_op | source)
XLA Modules:
  0.0 64.9 jit_solution(14162293528045630342)
XLA Ops:
  0.7 63.5 %conditional.1 = (f32[16,64,128]{2,1,0:T(8,128)S(1)}) conditional(s32[]{:T(128)} %clamp.3, (s32[1]{0:T(128)}, f32[16,64,128]{2,1,0:T(8,128)}, f32[3,16,64,128]{3,2,1,0:T(8,128)}, s32[3,16,64,128]{3,2,1,0:T(8,128)}, f32[16,64,128]{2,1,0:T(8,128)}) %tuple.17, (s32[1]{0:T(128)}, f32[16,64,128]{2,1,0:T(8,128)}, ...), branch_computations={%region_0.0_spmd, %region_1.0_spmd, %region_2.0_spmd, %region_3.0_... | conditional | bytes 8 | solution.py:265
  0.7 63.4 %slide0.1 = f32[16,64,128]{2,1,0:T(8,128)S(1)} custom-call(s32[1]{0:T(128)} %get-tuple-element.48.shear, f32[16,64,128]{2,1,0:T(8,128)} %get-tuple-element.87.conc, f32[3,16,64,128]{3,2,1,0:T(8,128)} %get-tuple-element.91.speed, s32[3,16,64,128]{3,2,1,0:T(8,128)} %get-tuple-element.95.signs, f32[16,64,128]{2,1,0:T(8,128)} %get-tuple-element.99.diff), custom_call_target="tpu_custom_call" | custom-call | tf_op jit(solution)/shard_map/cond/branch_0_fun/slide0/pallas_call | solution.py:233
  64.1 0.8 %copy.32 = f32[16,64,128]{2,1,0:T(8,128)} copy(f32[16,64,128]{2,1,0:T(8,128)S(1)} %get-tuple-element.70) | data formatting | bytes 1048576
where the time goes:
time: 65.5 us; the launch traced here: 64.9 us
  Pallas kernels  63.4 us (97%)
  local copies, waits for them, and re-layouts  0.8 us (1%)
  between operations  0.67 us (1%)
    pallas_call x1, Pallas kernels, run(): pl.pallas_call(functools.partial(kernel, hops, *counts), name=f'slide{hop...  63.4 us

commit v1 on v0

v1 whole, which is shorter than its diff:
```python
import functools

import jax
import jax.numpy as jnp
from jax import lax
from jax.experimental import pallas as pl
from jax.experimental.pallas import tpu as pltpu
from jax.sharding import PartitionSpec as P

STEPS = 8
time_step = 0.25
PAD = 8
MESH = pl.DeviceIdType.MESH


def kernel(
    hops, count_x, count_y, count_z,
    shear, conc, speed, signs, diff, out,
    field0, field1, coef, v_buf, s_buf, d_buf, low0, low1, high0, high1,
    y_out0, y_out1, y_in0, y_in1, z_out0, z_out1, z_in0, z_in1,
    load_sem, send_sem, recv_sem,
):
    nx, rows, lanes = conc.shape
    blocks = rows // 8
    span = 2 * nx
    per = lanes // span
    gx, gy, gz = (lax.axis_index(name) for name in ("gx", "gy", "gz"))
    low, high, field = (low0, low1), (high0, high1), (field0, field1)
    y_out, y_in = (y_out0, y_out1), (y_in0, y_in1)
    z_out, z_in = (z_out0, z_out1), (z_in0, z_in1)
    first, last = gx == 0, gx == count_x - 1
    body_rows = pl.ds(PAD, rows)

    def at(x, y):
        return {"gx": x, "gy": lax.rem(y + 2 * count_y, count_y)}

    up = (
        at(jnp.where(last, 0, gx + 1), gy - jnp.where(last, hops, 0)),
        at(0, gy - hops - 1),
    )
    down = (
        at(jnp.where(first, count_x - 1, gx - 1), gy + jnp.where(first, hops + 1, 0)),
        at(count_x - 1, gy + hops),
    )
    before_y, after_y = at(gx, gy - 1), at(gx, gy + 1)
    before_z = {"gz": lax.rem(gz + count_z - 1, count_z)}
    after_z = {"gz": lax.rem(gz + 1, count_z)}

    def remote(p, role, source, target, device):
        return pltpu.make_async_remote_copy(
            src_ref=source, dst_ref=target,
            send_sem=send_sem.at[p, role], recv_sem=recv_sem.at[p, role],
            device_id=device, device_id_type=MESH,
        )

    def copies(p):
        top = field[p].at[nx - 1, body_rows]
        bottom = field[p].at[0, body_rows]
        halves = (pl.ds(0, rows), pl.ds(rows, rows))
        return (
            remote(p, 0, top, low[p].at[halves[0]], up[0]),
            remote(p, 1, top, low[p].at[halves[1]], up[1]),
            remote(p, 2, bottom, high[p].at[halves[0]], down[0]),
            remote(p, 3, bottom, high[p].at[halves[1]], down[1]),
            remote(p, 4, y_out[p].at[0], y_in[p].at[1], before_y),
            remote(p, 5, y_out[p].at[1], y_in[p].at[0], after_y),
            remote(p, 6, z_out[p], z_in[p].at[1], before_z),
            remote(p, 7, z_out[p], z_in[p].at[0], after_z),
        )

    def send(p):
        c = copies(p)
        pl.when(last)(c[1].start)
        pl.when(first)(c[3].start)
        for role in (0, 2, 4, 5, 6, 7):
            c[role].start()

    lane = lax.broadcasted_iota(jnp.int32, (8, lanes), 1)
    even = lane % 2 == 0

    def turn(value, amount):
        amount = amount % lanes
        return pltpu.roll(value, amount, 1) if amount else value

    def record(q, packed, block, x, value):
        spot = span * (block % per) + 2 * x
        group = block // per
        moved = turn(value, spot + 1)
        packed[group] = jnp.where((lane == spot) | (lane == spot + 1), moved, packed[group])
        if block == 0:
            y_out[q][0, pl.ds(x, 1)] = value[:1]
        if block == blocks - 1:
            y_out[q][1, pl.ds(x, 1)] = value[7:]

    def store_packed(q, packed):
        for group, value in enumerate(packed):
            z_out[q][group] = value

    groups = blocks // per
    def nothing():
        return [jnp.zeros((8, lanes), jnp.float32) for _ in range(groups)]


    loads = (
        pltpu.make_async_copy(conc, field[0].at[:, body_rows], load_sem.at[0]),
        pltpu.make_async_copy(diff, d_buf, load_sem.at[1]),
        pltpu.make_async_copy(speed, v_buf, load_sem.at[2]),
        pltpu.make_async_copy(signs, s_buf, load_sem.at[3]),
    )
    for load in loads:
        load.start()

    barrier = pltpu.get_barrier_semaphore()

    def greet(device):
        pl.semaphore_signal(barrier, inc=1, device_id=device, device_id_type=MESH)

    for device in (up[0], down[0], before_y, after_y, before_z, after_z):
        greet(device)
    pl.when(last)(lambda: greet(up[1]))
    pl.when(first)(lambda: greet(down[1]))
    pl.semaphore_wait(barrier, 6 + jnp.where(first | last, 1, 0))

    loads[0].wait()

    packed = nothing()
    for block in range(blocks):
        for x in range(nx):
            record(0, packed, block, x, field[0][x, pl.ds(PAD + 8 * block, 8)])
    store_packed(0, packed)
    send(0)
    for load in loads[1:]:
        load.wait()

    def weigh(x, carry):
        d = time_step * d_buf[x]
        centre = 1.0 - 6.0 * d
        for axis in range(3):
            v = time_step * v_buf[axis, x]
            forward = s_buf[axis, x] > 0
            below = jnp.where(forward, v, 0.0)
            above = v - below
            coef[1 + 2 * axis, x] = d + below
            coef[2 + 2 * axis, x] = d - above
            centre = centre - below + above
        coef[0, x] = centre
        return carry

    lax.fori_loop(0, nx, weigh, 0)

    residue = lax.rem(shear[0], rows)
    low_start = jnp.where(first, residue, 0)
    high_start = jnp.where(last, rows - residue, 0)

    def step(p, more):
        q = 1 - p
        c = copies(p)
        old, new = field[p], field[q]
        c[6].wait_recv()
        c[7].wait_recv()
        sides = [
            jnp.where(even, z_in[p][0, group], turn(z_in[p][1, group], -2))
            for group in range(groups)
        ]
        packed = nothing()

        def cells(block, x, lower, here, upper):
            start = PAD + 8 * block
            part = pl.ds(8 * block, 8)
            side = turn(sides[block // per], -(span * (block % per) + 2 * x))
            z_minus = jnp.where(lane == 0, side, turn(here, 1))
            z_plus = jnp.where(lane == lanes - 1, side, turn(here, -1))
            total = (
                (coef[0, x, part] * here + coef[1, x, part] * lower)
                + (coef[2, x, part] * upper
                   + coef[3, x, part] * old[x, pl.ds(start - 1, 8)])
            ) + (
                (coef[4, x, part] * old[x, pl.ds(start + 1, 8)]
                 + coef[5, x, part] * z_minus)
                + coef[6, x, part] * z_plus
            )
            new[x, pl.ds(start, 8)] = total
            record(q, packed, block, x, total)

        def column(block):
            at_x = lambda x: old[x, pl.ds(PAD + 8 * block, 8)]
            lower, here = at_x(0), at_x(1)
            for x in range(1, nx - 1):
                upper = at_x(x + 1)
                cells(block, x, lower, here, upper)
                lower, here = here, upper

        for block in range(1, blocks - 1):
            column(block)
        c[4].wait_recv()
        c[5].wait_recv()
        for x in range(nx):
            old[x, pl.ds(PAD - 1, 1)] = y_in[p][0, pl.ds(x, 1)]
            old[x, pl.ds(PAD + rows, 1)] = y_in[p][1, pl.ds(x, 1)]
        column(0)
        column(blocks - 1)
        c[0].wait_recv()
        c[2].wait_recv()
        pl.when(first)(c[1].wait_recv)
        pl.when(last)(c[3].wait_recv)
        for block in range(blocks):
            at_x = lambda x: old[x, pl.ds(PAD + 8 * block, 8)]
            cells(block, 0, low[p][pl.ds(low_start + 8 * block, 8)], at_x(0), at_x(1))
            cells(block, nx - 1, at_x(nx - 2), at_x(nx - 1), high[p][pl.ds(high_start + 8 * block, 8)])
        store_packed(q, packed)
        for role in (0, 2, 4, 5, 6, 7):
            c[role].wait_send()
        pl.when(last)(c[1].wait_send)
        pl.when(first)(c[3].wait_send)
        if more is None:
            send(q)
        else:
            pl.when(more)(lambda: send(q))

    def pair(t, carry):
        step(0, None)
        step(1, t < STEPS // 2 - 1)
        return carry

    lax.fori_loop(0, STEPS // 2, pair, 0)
    store = pltpu.make_async_copy(field[STEPS % 2].at[:, body_rows], out, load_sem.at[0])
    store.start()
    store.wait()


def run(hops, counts, shear, conc, speed, signs, diff):
    nx, rows, lanes = conc.shape
    f32 = jnp.float32
    groups = (rows // 8) // (lanes // (2 * nx))
    anywhere = pl.BlockSpec(memory_space=pl.ANY)
    return pl.pallas_call(
        functools.partial(kernel, hops, *counts),
        name=f"slide{hops}",
        out_shape=jax.ShapeDtypeStruct(conc.shape, f32),
        in_specs=[pl.BlockSpec(memory_space=pltpu.SMEM)] + [anywhere] * 4,
        out_specs=anywhere,
        scratch_shapes=[
            pltpu.VMEM((nx, rows + 2 * PAD, lanes), f32),
            pltpu.VMEM((nx, rows + 2 * PAD, lanes), f32),
            pltpu.VMEM((7, nx, rows, lanes), f32),
            pltpu.VMEM((3, nx, rows, lanes), f32),
            pltpu.VMEM((3, nx, rows, lanes), jnp.int32),
            pltpu.VMEM((nx, rows, lanes), f32),
            pltpu.VMEM((2 * rows, lanes), f32),
            pltpu.VMEM((2 * rows, lanes), f32),
            pltpu.VMEM((2 * rows, lanes), f32),
            pltpu.VMEM((2 * rows, lanes), f32),
            *[pltpu.VMEM((2, nx, lanes), f32)] * 4,
            *[pltpu.VMEM((groups, 8, lanes), f32)] * 2,
            *[pltpu.VMEM((2, groups, 8, lanes), f32)] * 2,
            pltpu.SemaphoreType.DMA((4,)),
            pltpu.SemaphoreType.DMA((2, 8)),
            pltpu.SemaphoreType.DMA((2, 8)),
        ],
        compiler_params=pltpu.CompilerParams(collective_id=hops, has_side_effects=True),
    )(shear, conc, speed, signs, diff)


def body(concentration, speed, signs, diffusivity, shear):
    counts = tuple(lax.axis_size(name) for name in ("gx", "gy", "gz"))
    rows = concentration.shape[1]
    branches = [functools.partial(run, hops, counts) for hops in range(counts[1])]
    return lax.switch(
        lax.div(shear[0], rows), branches, shear, concentration, speed, signs, diffusivity
    )


def solution(mesh):
    placed = (
        P("gx", "gy", "gz"),
        P(None, "gx", "gy", "gz"),
        P(None, "gx", "gy", "gz"),
        P("gx", "gy", "gz"),
        P(),
    )
    return jax.shard_map(
        body, mesh=mesh, in_specs=placed, out_specs=P("gx", "gy", "gz"), check_vma=False
    )
```

time: 65.5 us -> 53 us (0.81)
  Pallas kernels: 63.4 us -> 50.9 us
    pallas_call x1, Pallas kernels: 63.4 us -> 50.9 us  [run(): pl.pallas_call(functools.partial(kernel, hops, *counts), name=f'slide{hop...]
where the time goes in v1:
time: 53 us; the launch traced here: 52.4 us
  Pallas kernels  50.9 us (96%)
  local copies, waits for them, and re-layouts  0.8 us (2%)
  between operations  0.67 us (1%)
    pallas_call x1, Pallas kernels, run(): pl.pallas_call(functools.partial(kernel, hops, *counts), name=f'slide{hop...  50.9 us

profile of v1, /device:TPU:0, one launch (start us, length us, event | category | flops | bytes accessed | tf_op | source)
XLA Modules:
  0.0 52.4 jit_solution(14609247801755215680)
XLA Ops:
  0.7 51.0 %conditional.1 = (f32[16,64,128]{2,1,0:T(8,128)S(1)}) conditional(s32[]{:T(128)} %clamp.3, (s32[1]{0:T(128)}, f32[16,64,128]{2,1,0:T(8,128)}, f32[3,16,64,128]{3,2,1,0:T(8,128)}, s32[3,16,64,128]{3,2,1,0:T(8,128)}, f32[16,64,128]{2,1,0:T(8,128)}) %tuple.17, (s32[1]{0:T(128)}, f32[16,64,128]{2,1,0:T(8,128)}, ...), branch_computations={%region_0.0_spmd, %region_1.0_spmd, %region_2.0_spmd, %region_3.0_... | conditional | bytes 8 | solution.py:268
  0.7 50.9 %slide1.1 = f32[16,64,128]{2,1,0:T(8,128)S(1)} custom-call(s32[1]{0:T(128)} %get-tuple-element.55.shear, f32[16,64,128]{2,1,0:T(8,128)} %get-tuple-element.88.conc, f32[3,16,64,128]{3,2,1,0:T(8,128)} %get-tuple-element.92.speed, s32[3,16,64,128]{3,2,1,0:T(8,128)} %get-tuple-element.96.signs, f32[16,64,128]{2,1,0:T(8,128)} %get-tuple-element.100.diff), custom_call_target="tpu_custom_call" | custom-call | tf_op jit(solution)/shard_map/cond/branch_1_fun/slide1/pallas_call | solution.py:236
  51.6 0.8 %copy.32 = f32[16,64,128]{2,1,0:T(8,128)} copy(f32[16,64,128]{2,1,0:T(8,128)S(1)} %get-tuple-element.70) | data formatting | bytes 1048576

commit v2 on v1

--- a/solution.py
+++ b/solution.py
@@ -70,10 +70,12 @@
 
     def send(p):
         c = copies(p)
+        for role in (6, 7, 4, 5):
+            c[role].start()
         pl.when(last)(c[1].start)
         pl.when(first)(c[3].start)
-        for role in (0, 2, 4, 5, 6, 7):
-            c[role].start()
+        c[0].start()
+        c[2].start()
 
     lane = lax.broadcasted_iota(jnp.int32, (8, lanes), 1)
     even = lane % 2 == 0
@@ -199,6 +201,10 @@
             old[x, pl.ds(PAD + rows, 1)] = y_in[p][1, pl.ds(x, 1)]
         column(0)
         column(blocks - 1)
+        for role in (0, 2, 4, 5, 6, 7):
+            c[role].wait_send()
+        pl.when(last)(c[1].wait_send)
+        pl.when(first)(c[3].wait_send)
         c[0].wait_recv()
         c[2].wait_recv()
         pl.when(first)(c[1].wait_recv)
@@ -208,10 +214,6 @@
             cells(block, 0, low[p][pl.ds(low_start + 8 * block, 8)], at_x(0), at_x(1))
             cells(block, nx - 1, at_x(nx - 2), at_x(nx - 1), high[p][pl.ds(high_start + 8 * block, 8)])
         store_packed(q, packed)
-        for role in (0, 2, 4, 5, 6, 7):
-            c[role].wait_send()
-        pl.when(last)(c[1].wait_send)
-        pl.when(first)(c[3].wait_send)
         if more is None:
             send(q)
         else:

time: 53 us -> 53.1 us (level)
  Pallas kernels: 50.9 us -> 51.5 us
    pallas_call x1, Pallas kernels: 50.9 us -> 51.5 us  [run(): pl.pallas_call(functools.partial(kernel, hops, *counts), name=f'slide{hop...]
where the time goes in v2:
time: 53.1 us; the launch traced here: 53 us
  Pallas kernels  51.5 us (97%)
  local copies, waits for them, and re-layouts  0.8 us (2%)
  between operations  0.67 us (1%)
    pallas_call x1, Pallas kernels, run(): pl.pallas_call(functools.partial(kernel, hops, *counts), name=f'slide{hop...  51.5 us

profile of v2, /device:TPU:0, one launch (start us, length us, event | category | flops | bytes accessed | tf_op | source)
XLA Modules:
  0.0 53.0 jit_solution(15161422949564263853)
XLA Ops:
  0.7 51.5 %conditional.1 = (f32[16,64,128]{2,1,0:T(8,128)S(1)}) conditional(s32[]{:T(128)} %clamp.3, (s32[1]{0:T(128)}, f32[16,64,128]{2,1,0:T(8,128)}, f32[3,16,64,128]{3,2,1,0:T(8,128)}, s32[3,16,64,128]{3,2,1,0:T(8,128)}, f32[16,64,128]{2,1,0:T(8,128)}) %tuple.17, (s32[1]{0:T(128)}, f32[16,64,128]{2,1,0:T(8,128)}, ...), branch_computations={%region_0.0_spmd, %region_1.0_spmd, %region_2.0_spmd, %region_3.0_... | conditional | bytes 8 | solution.py:270
  0.7 51.5 %slide3.1 = f32[16,64,128]{2,1,0:T(8,128)S(1)} custom-call(s32[1]{0:T(128)} %get-tuple-element.65.shear, f32[16,64,128]{2,1,0:T(8,128)} %get-tuple-element.90.conc, f32[3,16,64,128]{3,2,1,0:T(8,128)} %get-tuple-element.94.speed, s32[3,16,64,128]{3,2,1,0:T(8,128)} %get-tuple-element.98.signs, f32[16,64,128]{2,1,0:T(8,128)} %get-tuple-element.102.diff), custom_call_target="tpu_custom_call" | custom-call | tf_op jit(solution)/shard_map/cond/branch_3_fun/slide3/pallas_call | solution.py:238
  52.2 0.8 %copy.32 = f32[16,64,128]{2,1,0:T(8,128)} copy(f32[16,64,128]{2,1,0:T(8,128)S(1)} %get-tuple-element.70) | data formatting | bytes 1048576
